TPU v7x, 256 devices: a whole 4x4x8 slice. The times are simulated.
256 devices in a mesh: grp: 4 (over y), dev: 64 (over x, z, core).
Axes of the slice: x: 4, y: 4, z: 8, core: 2. Of those that a mesh axis runs over, the one named last changes fastest.
Arguments:
- pool_rows: bfloat16 [262144, 1024], P(('grp', 'dev')), may hold values from -6 to 6
- sample_index: int32 [262144], P(('grp', 'dev')), may hold values from 0 to 262143, as said below
- cluster_id: int32 [262144], P(('grp', 'dev')), may hold values from 0 to 511, as said below
- child_id: int32 [262144], P(('grp', 'dev')), may hold values from 0 to 7
- old_centroids: float32 [512, 8, 1024], P('dev'), may hold values from -6 to 6
Outputs:
- centroids: float32 [512, 8, 1024], P('dev')
- child_counts: int32 [512, 8], P('dev')
Inputs may be any that keep to these rules, and one draw needn't show every extreme that they name: Sample i takes a pool row of its own aligned block of 1024 rows: sample_index[i] // 1024 == i // 1024. `cluster_id`: in each aligned block of 1024 samples (the rows of one device) the 2 clusters o * 2 to o * 2 + 1 of any owner o are named at most 8 times together, and one cluster, the same in every block, is named exactly 8 times in every block.
All inputs are finite; a program needn't handle non-finite values.
Results may differ from a plain program's by a relative error of at most 0.0003.
Values may be sent and summed in bfloat16 or wider, within the bound.
A program may use at most 64 MiB of HBM per device.

v0:
```python
import math
import jax
import jax.numpy as jnp
from jax import lax
from jax.sharding import PartitionSpec as P


def side_by_side(arrays, axis, dim, along):
    widths = [math.prod(a.shape[along:]) for a in arrays]
    both = jnp.concatenate(
        [a.reshape(*a.shape[:along], w) for a, w in zip(arrays, widths)], axis=along
    )
    filled = lax.all_gather(both, axis, axis=dim, tiled=True)
    parts = jnp.split(filled, [sum(widths[:k]) for k in range(1, len(widths))], axis=along)
    return tuple(
        (b.reshape(*filled.shape[:along], *a.shape[along:]) for a, b in zip(arrays, parts))
    )


def segment_totals(rows, segment, segments):
    onehot = (jnp.arange(segments, dtype=jnp.int32)[:, None] == segment[None, :]).astype(
        jnp.bfloat16
    )
    sums = jnp.dot(onehot, rows, preferred_element_type=jnp.float32)
    counts = jnp.sum(onehot.astype(jnp.float32), axis=1)
    return (sums, counts)


def rank_within(keys_here):
    positions = jnp.arange(keys_here.shape[0], dtype=jnp.int32)
    matches = keys_here[:, None] == keys_here[None, :]
    earlier = positions[None, :] < positions[:, None]
    return jnp.sum(matches & earlier, axis=1)


def per_device(pool_rows, sample_index, cluster_id, child_id, old_centroids):
    rows_dev, row_width = pool_rows.shape
    block_clusters, kinds = (old_centroids.shape[0], old_centroids.shape[1])
    groups = lax.axis_size("grp")
    owners = lax.axis_size("dev")
    owned = block_clusters // groups
    clusters = block_clusters * owners
    most = 4 * rows_dev // clusters
    sample = pool_rows[sample_index % rows_dev]
    holder_table = cluster_id // owned
    slot_of = holder_table * most + rank_within(holder_table)
    total_slots = clusters // owned * most
    label_of = cluster_id % owned * kinds + child_id
    buffer = jnp.zeros((total_slots, row_width), jnp.bfloat16).at[slot_of].set(sample)
    labels = jnp.full((total_slots,), -1, jnp.int32).at[slot_of].set(label_of)
    shaped = buffer.reshape(owners, groups, most, row_width)
    shaped_labels = labels.reshape(owners, groups, most)
    arrived, arrived_labels = (
        lax.all_to_all(
            lax.all_to_all(shaped, "dev", split_axis=0, concat_axis=0, tiled=True),
            "grp",
            split_axis=1,
            concat_axis=1,
            tiled=True,
        ),
        lax.all_to_all(
            lax.all_to_all(shaped_labels, "dev", split_axis=0, concat_axis=0, tiled=True),
            "grp",
            split_axis=1,
            concat_axis=1,
            tiled=True,
        ),
    )
    sums, counts = segment_totals(
        arrived.reshape(-1, row_width), arrived_labels.reshape(-1), owned * kinds
    )
    group_index = lax.axis_index("grp")
    mine = lax.dynamic_slice_in_dim(old_centroids, group_index * owned, owned, 0)
    counts_owned = counts.reshape(owned, kinds)
    fresh = (sums.reshape(owned, kinds, row_width) + mine) / (counts_owned[:, :, None] + 1.0)
    centroids, new_counts = side_by_side((fresh, counts_owned), "grp", 0, 2)
    return (centroids, new_counts.astype(jnp.int32))


def solution(mesh):
    placed = (
        P(("grp", "dev"), None),
        P(("grp", "dev")),
        P(("grp", "dev")),
        P(("grp", "dev")),
        P("dev", None, None),
    )
    return jax.shard_map(
        per_device,
        mesh=mesh,
        in_specs=placed,
        out_specs=(P("dev", None, None), P("dev", None)),
        check_vma=False,
    )
```

profile of v0, /device:TPU:2, one launch (start us, length us, event | category | flops | bytes accessed | tf_op | source)
XLA Modules:
  0.0 222.8 jit_solution(11543515831146436987)
XLA Ops:
  0.6 0.0 copy-start
  0.6 0.8 add_select_fusion.2
  1.5 0.5 convert_reduce_fusion
  2.0 0.7 fusion.10
  2.8 4.3 %scatter_custom_fusion = s32[2048]{0:T(1024)S(1)} fusion(s32[1024]{0:T(1024)S(1)} %get-tuple-element.3, s32[1024]{0:T(1024)S(1)} %get-tuple-element.2, s32[]{:T(128)} %constant.47.clone.1), kind=kCustom, calls=%fused_computation.34 | custom fusion | bytes 8196 | tf_op jit(solution)/shard_map/scatter | solution.py:50
  7.1 0.8 reshape.46
  7.9 12.0 %all-to-all-start = ((s32[64,4,8]{2,1,0:T(4,128)}), s32[64,4,8]{2,1,0:T(4,128)S(1)}, u32[]{:S(2)}, u32[]{:S(2)}) async-start(s32[64,4,8]{2,1,0:T(4,128)} %reshape.46), calls=%async_computation | async-start | bytes 262144 | tf_op jit(solution)/shard_map/all_to_all | solution.py:62
  20.0 15.3 %scatter_custom_fusion.1 = bf16[2048,1024]{1,0:T(8,128)(2,1)} fusion(s32[1024]{0:T(1024)S(1)} %get-tuple-element.3, bf16[1024,1024]{1,0:T(8,128)(2,1)S(1)} %copy-done, s32[1024]{0:T(1024)S(1)} %get-tuple-element.4, bf16[]{:T(256)} %constant.52.clone.1), kind=kCustom, calls=%fused_computation.6 | custom fusion | bytes 4194306 | tf_op jit(solution)/shard_map/scatter | solution.py:49
  35.3 0.0 all-to-all-done
  35.3 10.5 %all-to-all-start.2 = ((bf16[64,4,8,1024]{3,2,1,0:T(8,128)(2,1)}), bf16[64,4,8,1024]{3,2,1,0:T(8,128)(2,1)}, u32[]{:S(2)}, u32[]{:S(2)}) async-start(bf16[64,4,8,1024]{3,2,1,0:T(8,128)(2,1)} %bitcast.10), calls=%async_computation.2 | async-start | bytes 8388608 | tf_op jit(solution)/shard_map/all_to_all | solution.py:55
  45.8 0.1 copy.20
  45.9 0.7 reshape.85
  46.6 94.0 %all-to-all-done.2 = bf16[64,4,8,1024]{3,2,1,0:T(8,128)(2,1)} async-done(((bf16[64,4,8,1024]{3,2,1,0:T(8,128)(2,1)}), bf16[64,4,8,1024]{3,2,1,0:T(8,128)(2,1)}, u32[]{:S(2)}, u32[]{:S(2)}) %all-to-all-start.2) | async-done | bytes 4194336 | tf_op jit(solution)/shard_map/all_to_all | solution.py:55
  140.5 4.5 %all-to-all-start.1 = ((s32[4,1,512]{2,1,0:T(1,128)}), s32[4,1,512]{2,1,0:T(1,128)S(1)}, u32[]{:S(2)}, u32[]{:S(2)}) async-start(s32[4,1,512]{2,1,0:T(1,128)} %reshape.85), calls=%async_computation.1 | async-start | bytes 16384 | tf_op jit(solution)/shard_map/all_to_all | solution.py:61
  145.0 4.8 %copy.22 = bf16[64,4,8,1024]{3,2,0,1:T(8,128)(2,1)} copy(bf16[64,4,8,1024]{3,2,1,0:T(8,128)(2,1)} %all-to-all-done.2) | data formatting | bytes 8388608 | tf_op jit(solution)/shard_map/all_to_all | solution.py:55
  149.8 0.6 all-to-all-done.1
  150.3 4.9 %all-to-all-start.3 = ((bf16[64,4,8,1024]{3,2,0,1:T(8,128)(2,1)}), bf16[64,4,8,1024]{3,2,0,1:T(8,128)(2,1)}, u32[]{:S(2)}, u32[]{:S(2)}) async-start(bf16[64,4,8,1024]{3,2,0,1:T(8,128)(2,1)} %copy.22), calls=%async_computation.3 | async-start | bytes 8388608 | tf_op jit(solution)/shard_map/all_to_all | solution.py:54
  155.2 0.5 broadcast.69
  155.7 0.7 reduce
  156.4 0.1 reshape.86
  156.5 0.1 copy.21
  156.6 0.2 eq.55
  156.7 0.1 convert_reduce_fusion.1
  156.9 0.1 broadcast_in_dim_reshape.5
  157.0 0.1 add.55
  157.1 47.7 %all-to-all-done.3 = bf16[64,4,8,1024]{3,2,0,1:T(8,128)(2,1)} async-done(((bf16[64,4,8,1024]{3,2,0,1:T(8,128)(2,1)}), bf16[64,4,8,1024]{3,2,0,1:T(8,128)(2,1)}, u32[]{:S(2)}, u32[]{:S(2)}) %all-to-all-start.3) | async-done | bytes 4194336 | tf_op jit(solution)/shard_map/all_to_all | solution.py:54
  204.7 2.6 %copy.23 = bf16[64,4,8,1024]{3,2,1,0:T(8,128)(2,1)S(1)} copy(bf16[64,4,8,1024]{3,2,0,1:T(8,128)(2,1)} %all-to-all-done.3) | data formatting | bytes 8388608 | tf_op jit(solution)/shard_map/all_to_all | solution.py:54
  207.4 1.5 fusion.4
  208.9 12.4 %all_gather.3 = f32[8,8,1025]{2,1,0:T(8,128)S(1)} all-gather(f32[2,8,1025]{2,1,0:T(8,128)S(1)} %pad_maximum_fusion), channel_id=1, replica_groups=mesh['grp'=4,'dev'=64] {'grp'}, dimensions={0}, use_global_device_ids=true | all-gather | bytes 328000 | tf_op jit(solution)/shard_map/all_gather | solution.py:13
  221.4 0.7 split.8
  222.1 0.1 copy.26
  222.2 0.6 convert_bitcast_fusion
  (5 shorter events, 0.0 us)
Async XLA Ops:
  0.6 19.3 %copy-start = (bf16[1024,1024]{1,0:T(8,128)(2,1)S(1)}, bf16[1024,1024]{1,0:T(8,128)(2,1)}, u32[]{:S(2)}) copy-start(bf16[1024,1024]{1,0:T(8,128)(2,1)} %param.5) | copy-start | bytes 6291460
  7.9 27.4 %all-to-all-start = ((s32[64,4,8]{2,1,0:T(4,128)}), s32[64,4,8]{2,1,0:T(4,128)S(1)}, u32[]{:S(2)}, u32[]{:S(2)}) async-start(s32[64,4,8]{2,1,0:T(4,128)} %reshape.46), calls=%async_computation | async-start | bytes 262144 | tf_op jit(solution)/shard_map/all_to_all | solution.py:62
  35.3 105.3 %all-to-all-start.2 = ((bf16[64,4,8,1024]{3,2,1,0:T(8,128)(2,1)}), bf16[64,4,8,1024]{3,2,1,0:T(8,128)(2,1)}, u32[]{:S(2)}, u32[]{:S(2)}) async-start(bf16[64,4,8,1024]{3,2,1,0:T(8,128)(2,1)} %bitcast.10), calls=%async_computation.2 | async-start | bytes 8388608 | tf_op jit(solution)/shard_map/all_to_all | solution.py:55
  140.5 9.8 %all-to-all-start.1 = ((s32[4,1,512]{2,1,0:T(1,128)}), s32[4,1,512]{2,1,0:T(1,128)S(1)}, u32[]{:S(2)}, u32[]{:S(2)}) async-start(s32[4,1,512]{2,1,0:T(1,128)} %reshape.85), calls=%async_computation.1 | async-start | bytes 16384 | tf_op jit(solution)/shard_map/all_to_all | solution.py:61
  150.3 54.4 %all-to-all-start.3 = ((bf16[64,4,8,1024]{3,2,0,1:T(8,128)(2,1)}), bf16[64,4,8,1024]{3,2,0,1:T(8,128)(2,1)}, u32[]{:S(2)}, u32[]{:S(2)}) async-start(bf16[64,4,8,1024]{3,2,0,1:T(8,128)(2,1)} %copy.22), calls=%async_computation.3 | async-start | bytes 8388608 | tf_op jit(solution)/shard_map/all_to_all | solution.py:54
where the time goes:
time: 223 us
  waiting for transfers between devices  142 us (64%)
  starting transfers between devices  31.9 us (14%)
  local copies, waits for them, and re-layouts  30.5 us (14%)
  blocking collectives  12.4 us (6%)
  other arithmetic  3.54 us (2%)
    all_to_all x1, waiting for transfers between devices, per_device(): lax.all_to_all(shaped, 'dev', split_axis=0, concat_axis=0, tiled=True)  94 us
    all_to_all x1, waiting for transfers between devices, per_device(): lax.all_to_all(lax.all_to_all(shaped, 'dev', split_axis=0, concat_axis=0,...  47.7 us
    scatter x1, local copies, waits for them, and re-layouts, per_device(): jnp.zeros((total_slots, row_width), jnp.bfloat16).at[slot_of].set(sample)  15.3 us
    all_gather x1, blocking collectives, side_by_side(): filled = lax.all_gather(both, axis, axis=dim, tiled=True)  12.4 us
    all_to_all x1, starting transfers between devices, per_device(): lax.all_to_all(shaped_labels, 'dev', split_axis=0, concat_axis=0, tiled=T...  12 us
    all_to_all x1, starting transfers between devices, per_device(): lax.all_to_all(shaped, 'dev', split_axis=0, concat_axis=0, tiled=True)  10.5 us
    all_to_all x1, starting transfers between devices, per_device(): lax.all_to_all(lax.all_to_all(shaped, 'dev', split_axis=0, concat_axis=0,...  4.86 us
    all_to_all x1, local copies, waits for them, and re-layouts, per_device(): lax.all_to_all(shaped, 'dev', split_axis=0, concat_axis=0, tiled=True)  4.75 us
  transfers between devices with their start and end apart: 4, of which 3 were waited for; matrix products, arithmetic and copies ran while one was open for 10% of the time, Pallas kernels for 0%

commit v1 on v0

--- a/solution.py
+++ b/solution.py
@@ -3,6 +3,28 @@
 import jax.numpy as jnp
 from jax import lax
 from jax.sharding import PartitionSpec as P
+
+
+def cut_along(x, dim, peers):
+    before, after = (x.shape[:dim], x.shape[dim + 1 :])
+    return jnp.moveaxis(x.reshape(*before, peers, -1, *after), dim, 0)
+
+
+def in_order(blocks, dim):
+    blocks = jnp.moveaxis(blocks, 0, dim)
+    shape = blocks.shape
+    return blocks.reshape(*shape[:dim], shape[dim] * shape[dim + 1], *shape[dim + 2 :])
+
+
+def swapped_with_each(x, axis, split_dim, concat_dim):
+    devices, index = (lax.axis_size(axis), lax.axis_index(axis))
+    blocks = cut_along(x, split_dim, devices)
+    finished = [blocks[index]]
+    for step in range(1, devices):
+        sent = blocks[index ^ step]
+        finished.append(lax.ppermute(sent, axis, [(i, i ^ step) for i in range(devices)]))
+    blocks = jnp.stack(finished)[index ^ jnp.arange(devices)]
+    return in_order(blocks, concat_dim)
 
 
 def side_by_side(arrays, axis, dim, along):
@@ -51,12 +73,8 @@
     shaped = buffer.reshape(owners, groups, most, row_width)
     shaped_labels = labels.reshape(owners, groups, most)
     arrived, arrived_labels = (
-        lax.all_to_all(
-            lax.all_to_all(shaped, "dev", split_axis=0, concat_axis=0, tiled=True),
-            "grp",
-            split_axis=1,
-            concat_axis=1,
-            tiled=True,
+        swapped_with_each(
+            lax.all_to_all(shaped, "dev", split_axis=0, concat_axis=0, tiled=True), "grp", 1, 1
         ),
         lax.all_to_all(
             lax.all_to_all(shaped_labels, "dev", split_axis=0, concat_axis=0, tiled=True),

time: 223 us -> 212 us (0.951)
  waiting for transfers between devices: 142 us -> 127 us
  local copies, waits for them, and re-layouts: 30.5 us -> 34.6 us
  starting transfers between devices: 31.9 us -> 27.8 us
  other arithmetic: 3.54 us -> 7.14 us
    all_to_all x1 -> x0, waiting for transfers between devices: 47.7 us -> none  [per_device(): lax.all_to_all(lax.all_to_all(shaped, 'dev', split_axis=0, concat_axis=0,...]
    all_to_all x1, waiting for transfers between devices: 0.57 us -> 23.2 us  [per_device(): lax.all_to_all(lax.all_to_all(shaped_labels, 'dev', split_axis=0, concat_...]
    all_to_all x1, waiting for transfers between devices: 0.01 us -> 9.34 us  [per_device(): lax.all_to_all(shaped_labels, 'dev', split_axis=0, concat_axis=0, tiled=T...]
    all_to_all x2 -> x0, local copies, waits for them, and re-layouts: 7.38 us -> none  [the longest x1 4.75 us: per_device(): lax.all_to_all(shaped, 'dev', split_axis=0, concat_axis=0, tiled=True)]
    all_to_all x1, starting transfers between devices: 12 us -> 6.65 us  [per_device(): lax.all_to_all(shaped_labels, 'dev', split_axis=0, concat_axis=0, tiled=T...]
    gather x0 -> x1, local copies, waits for them, and re-layouts: none -> 4.97 us  [swapped_with_each(): blocks = jnp.stack(finished)[index ^ jnp.arange(devices)]]
    all_to_all x1 -> x0, starting transfers between devices: 4.86 us -> none  [per_device(): lax.all_to_all(lax.all_to_all(shaped, 'dev', split_axis=0, concat_axis=0,...]
    ppermute x0 -> x3, starting transfers between devices: none -> 4.7 us  [swapped_with_each(): lax.ppermute(sent, axis, [(i, i ^ step) for i in range(devices)])]
  transfers between devices with their start and end apart: 4 -> 6, of which waited for: 3 -> 3; matrix products, arithmetic and copies ran while one was open for 10% -> 4% of each run, Pallas kernels for 0% -> 0%
where the time goes in v1:
time: 212 us
  waiting for transfers between devices  127 us (60%)
  local copies, waits for them, and re-layouts  34.6 us (16%)
  starting transfers between devices  27.8 us (13%)
  blocking collectives  12.6 us (6%)
  other arithmetic  7.14 us (3%)
    all_to_all x1, waiting for transfers between devices, per_device(): lax.all_to_all(shaped, 'dev', split_axis=0, concat_axis=0, tiled=True)  94.7 us
    all_to_all x1, waiting for transfers between devices, per_device(): lax.all_to_all(lax.all_to_all(shaped_labels, 'dev', split_axis=0, concat_...  23.2 us
    scatter x1, local copies, waits for them, and re-layouts, per_device(): jnp.zeros((total_slots, row_width), jnp.bfloat16).at[slot_of].set(sample)  15.3 us
    all_gather x1, blocking collectives, side_by_side(): filled = lax.all_gather(both, axis, axis=dim, tiled=True)  12.6 us
    all_to_all x1, starting transfers between devices, per_device(): lax.all_to_all(shaped, 'dev', split_axis=0, concat_axis=0, tiled=True)  12.2 us
    all_to_all x1, waiting for transfers between devices, per_device(): lax.all_to_all(shaped_labels, 'dev', split_axis=0, concat_axis=0, tiled=T...  9.34 us
    all_to_all x1, starting transfers between devices, per_device(): lax.all_to_all(shaped_labels, 'dev', split_axis=0, concat_axis=0, tiled=T...  6.65 us
    gather x1, local copies, waits for them, and re-layouts, swapped_with_each(): blocks = jnp.stack(finished)[index ^ jnp.arange(devices)]  4.97 us
  transfers between devices with their start and end apart: 6, of which 3 were waited for; matrix products, arithmetic and copies ran while one was open for 4% of the time, Pallas kernels for 0%

profile of v1, /device:TPU:2, one launch (start us, length us, event | category | flops | bytes accessed | tf_op | source)
XLA Modules:
  0.0 211.7 jit_solution(5443434539753153519)
XLA Ops:
  0.6 0.8 add_select_fusion.2
  1.5 0.5 convert_reduce_fusion
  2.0 0.7 fusion.10
  2.8 15.3 %scatter_custom_fusion.1 = bf16[2048,1024]{1,0:T(8,128)(2,1)} fusion(s32[1024]{0:T(1024)S(1)} %get-tuple-element.7, bf16[1024,1024]{1,0:T(8,128)(2,1)S(1)} %copy-done, s32[1024]{0:T(1024)S(1)} %get-tuple-element.8, bf16[]{:T(256)} %constant.57.clone.1), kind=kCustom, calls=%fused_computation.8 | custom fusion | bytes 4194306 | tf_op jit(solution)/shard_map/scatter | solution.py:71
  18.1 12.2 %all-to-all-start.2 = ((bf16[64,4,8,1024]{3,2,1,0:T(8,128)(2,1)}), bf16[64,4,8,1024]{3,2,1,0:T(8,128)(2,1)}, u32[]{:S(2)}, u32[]{:S(2)}) async-start(bf16[64,4,8,1024]{3,2,1,0:T(8,128)(2,1)} %bitcast.28), calls=%async_computation.2 | async-start | bytes 8388608 | tf_op jit(solution)/shard_map/all_to_all | solution.py:77
  30.3 94.7 %all-to-all-done.2 = bf16[64,4,8,1024]{3,2,1,0:T(8,128)(2,1)} async-done(((bf16[64,4,8,1024]{3,2,1,0:T(8,128)(2,1)}), bf16[64,4,8,1024]{3,2,1,0:T(8,128)(2,1)}, u32[]{:S(2)}, u32[]{:S(2)}) %all-to-all-start.2) | async-done | bytes 4194336 | tf_op jit(solution)/shard_map/all_to_all | solution.py:77
  125.0 3.9 %dynamic-slice_bitcast_fusion.3 = (bf16[1,64,1,8,1024]{4,3,1,0,2:T(8,128)(2,1)S(1)}, bf16[64,1,8,1024]{3,2,0,1:T(8,128)(2,1)}, bf16[64,1,8,1024]{3,2,0,1:T(8,128)(2,1)}, bf16[64,1,8,1024]{3,2,0,1:T(8,128)(2,1)}) fusion(bf16[64,4,8,1024]{3,2,1,0:T(8,128)(2,1)} %all-to-all-done.2, s32[]{:T(128)S(6)} %select_n.53, s32[]{:T(128)S(6)} %select_n.55, ...), kind=kLoop, calls=%fused_computation.16 | loop fusion | bytes 8388624 | tf_op jit(solution)/shard_map/dynamic_slice | solution.py:22
  128.9 1.6 collective-permute-start
  130.5 2.9 %collective-permute-start.1 = (bf16[64,1,8,1024]{3,2,0,1:T(8,128)(2,1)}, bf16[64,1,8,1024]{3,2,0,1:T(8,128)(2,1)}, u32[]{:S(2)}, u32[]{:S(2)}) collective-permute-start(bf16[64,1,8,1024]{3,2,0,1:T(8,128)(2,1)} %get-tuple-element.3), channel_id=1, source_target_pairs={{0,128},{64,192},{128,0},{192,64},{1,129},{65,193},{129,1},{193,65... | collective-permute-start | bytes 3145736 | tf_op jit(solution)/shard_map/ppermute | solution.py:25
  133.4 0.2 collective-permute-start.2
  133.6 4.3 %scatter_custom_fusion = s32[2048]{0:T(1024)S(1)} fusion(s32[1024]{0:T(1024)S(1)} %get-tuple-element.7, s32[1024]{0:T(1024)S(1)} %get-tuple-element.6, s32[]{:T(128)} %constant.52.clone.1), kind=kCustom, calls=%fused_computation.41 | custom fusion | bytes 8196 | tf_op jit(solution)/shard_map/scatter | solution.py:72
  138.0 0.8 reshape.75
  138.8 6.6 %all-to-all-start = ((s32[64,4,8]{2,1,0:T(4,128)}), s32[64,4,8]{2,1,0:T(4,128)S(1)}, u32[]{:S(2)}, u32[]{:S(2)}) async-start(s32[64,4,8]{2,1,0:T(4,128)} %reshape.75), calls=%async_computation | async-start | bytes 262144 | tf_op jit(solution)/shard_map/all_to_all | solution.py:80
  145.5 9.3 %all-to-all-done = s32[64,4,8]{2,1,0:T(4,128)S(1)} async-done(((s32[64,4,8]{2,1,0:T(4,128)}), s32[64,4,8]{2,1,0:T(4,128)S(1)}, u32[]{:S(2)}, u32[]{:S(2)}) %all-to-all-start) | async-done | bytes 8224 | tf_op jit(solution)/shard_map/all_to_all | solution.py:80
  154.9 0.7 reshape.123
  155.6 4.3 %all-to-all-start.1 = ((s32[4,1,512]{2,1,0:T(1,128)}), s32[4,1,512]{2,1,0:T(1,128)S(1)}, u32[]{:S(2)}, u32[]{:S(2)}) async-start(s32[4,1,512]{2,1,0:T(1,128)} %reshape.123), calls=%async_computation.1 | async-start | bytes 16384 | tf_op jit(solution)/shard_map/all_to_all | solution.py:79
  159.9 23.2 %all-to-all-done.1 = s32[4,1,512]{2,1,0:T(1,128)S(1)} async-done(((s32[4,1,512]{2,1,0:T(1,128)}), s32[4,1,512]{2,1,0:T(1,128)S(1)}, u32[]{:S(2)}, u32[]{:S(2)}) %all-to-all-start.1) | async-done | bytes 8224 | tf_op jit(solution)/shard_map/all_to_all | solution.py:79
  183.1 0.5 broadcast.110
  183.6 0.7 reduce
  184.4 0.1 copy.27
  184.5 0.2 eq.55
  184.6 0.1 convert_reduce_fusion.1
  184.8 0.1 broadcast_in_dim_reshape.5
  184.9 0.1 add.82
  185.0 3.6 %maximum_bitcast_fusion = bf16[4,64,8,1024]{3,2,1,0:T(8,128)(2,1)} fusion(bf16[1,64,1,8,1024]{4,3,1,0,2:T(8,128)(2,1)} %bitcast.4, bf16[1,64,1,8,1024]{4,3,1,0,2:T(8,128)(2,1)} %bitcast.3, bf16[1,64,1,8,1024]{4,3,1,0,2:T(8,128)(2,1)} %bitcast.2, bf16[1,64,1,8,1024]{4,3,1,0,2:T(8,128)(2,1)S(1)} %get-tuple-element.2), kind=kLoop, calls=%fused_computation.4 | loop fusion | flops 6291456 | bytes 8388608 | tf_op jit(solution)/shard_map/stack | solution.py:26
  188.5 5.0 %gather_fusion = bf16[4,64,8,1024]{3,2,1,0:T(8,128)(2,1)} fusion(bf16[4,64,8,1024]{3,2,1,0:T(8,128)(2,1)} %maximum_bitcast_fusion, s32[1024]{0:T(1024)S(1)} %pad_clamp_fusion), kind=kCustom, calls=%fused_computation.1 | custom fusion | bytes 8388624 | tf_op jit(solution)/shard_map/gather | solution.py:26
  193.5 2.6 %copy.31 = bf16[64,4,1,8,1024]{4,3,1,0,2:T(8,128)(2,1)S(1)} copy(bf16[64,4,1,8,1024]{4,3,0,1,2:T(8,128)(2,1)} %bitcast.29) | data formatting | bytes 8388608 | tf_op jit(solution)/shard_map/transpose | solution.py:14
  196.2 1.5 fusion.4
  197.7 12.6 %all_gather.3 = f32[8,8,1025]{2,1,0:T(8,128)S(1)} all-gather(f32[2,8,1025]{2,1,0:T(8,128)S(1)} %pad_maximum_fusion), channel_id=1, replica_groups=mesh['grp'=4,'dev'=64] {'grp'}, dimensions={0}, use_global_device_ids=true | all-gather | bytes 328000 | tf_op jit(solution)/shard_map/all_gather | solution.py:35
  210.3 0.7 split.8
  211.0 0.1 copy.37
  211.1 0.6 convert_bitcast_fusion
  (13 shorter events, 0.2 us)
Async XLA Ops:
  0.6 2.1 %copy-start = (bf16[1024,1024]{1,0:T(8,128)(2,1)S(1)}, bf16[1024,1024]{1,0:T(8,128)(2,1)}, u32[]{:S(2)}) copy-start(bf16[1024,1024]{1,0:T(8,128)(2,1)} %param.5) | copy-start | bytes 6291460
  18.1 107.0 %all-to-all-start.2 = ((bf16[64,4,8,1024]{3,2,1,0:T(8,128)(2,1)}), bf16[64,4,8,1024]{3,2,1,0:T(8,128)(2,1)}, u32[]{:S(2)}, u32[]{:S(2)}) async-start(bf16[64,4,8,1024]{3,2,1,0:T(8,128)(2,1)} %bitcast.28), calls=%async_computation.2 | async-start | bytes 8388608 | tf_op jit(solution)/shard_map/all_to_all | solution.py:77
  128.9 56.0 %collective-permute-start = (bf16[64,1,8,1024]{3,2,0,1:T(8,128)(2,1)}, bf16[64,1,8,1024]{3,2,0,1:T(8,128)(2,1)}, u32[]{:S(2)}, u32[]{:S(2)}) collective-permute-start(bf16[64,1,8,1024]{3,2,0,1:T(8,128)(2,1)} %get-tuple-element.4), channel_id=1, source_target_pairs={{0,64},{64,0},{128,192},{192,128},{1,65},{65,1},{129,193},{193,129... | collective-permute-start | bytes 3145736 | tf_op jit(solution)/shard_map/ppermute | solution.py:25
  130.5 54.4 %collective-permute-start.1 = (bf16[64,1,8,1024]{3,2,0,1:T(8,128)(2,1)}, bf16[64,1,8,1024]{3,2,0,1:T(8,128)(2,1)}, u32[]{:S(2)}, u32[]{:S(2)}) collective-permute-start(bf16[64,1,8,1024]{3,2,0,1:T(8,128)(2,1)} %get-tuple-element.3), channel_id=1, source_target_pairs={{0,128},{64,192},{128,0},{192,64},{1,129},{65,193},{129,1},{193,65... | collective-permute-start | bytes 3145736 | tf_op jit(solution)/shard_map/ppermute | solution.py:25
  133.4 51.5 %collective-permute-start.2 = (bf16[64,1,8,1024]{3,2,0,1:T(8,128)(2,1)}, bf16[64,1,8,1024]{3,2,0,1:T(8,128)(2,1)}, u32[]{:S(2)}, u32[]{:S(2)}) collective-permute-start(bf16[64,1,8,1024]{3,2,0,1:T(8,128)(2,1)} %get-tuple-element.5), channel_id=1, source_target_pairs={{0,192},{64,128},{128,64},{192,0},{1,193},{65,129},{129,65},{193,1... | collective-permute-start | bytes 3145736 | tf_op jit(solution)/shard_map/ppermute | solution.py:25
  138.8 16.0 %all-to-all-start = ((s32[64,4,8]{2,1,0:T(4,128)}), s32[64,4,8]{2,1,0:T(4,128)S(1)}, u32[]{:S(2)}, u32[]{:S(2)}) async-start(s32[64,4,8]{2,1,0:T(4,128)} %reshape.75), calls=%async_computation | async-start | bytes 262144 | tf_op jit(solution)/shard_map/all_to_all | solution.py:80
  155.6 27.5 %all-to-all-start.1 = ((s32[4,1,512]{2,1,0:T(1,128)}), s32[4,1,512]{2,1,0:T(1,128)S(1)}, u32[]{:S(2)}, u32[]{:S(2)}) async-start(s32[4,1,512]{2,1,0:T(1,128)} %reshape.123), calls=%async_computation.1 | async-start | bytes 16384 | tf_op jit(solution)/shard_map/all_to_all | solution.py:79
